TPU v7x, 32 devices: a whole 2x2x4 slice. The times are simulated.
32 devices in a mesh: grp: 2 (over y), seq: 8 (over z, x), head: 2 (over core).
Axes of the slice: x: 2, y: 2, z: 4, core: 2. Of those that a mesh axis runs over, the one named last changes fastest.
Arguments:
- query_rows: bfloat16 [16, 32, 128], P('grp', 'head'), parts along dimension 0, may hold values from -100 to 100
- cache_keys: bfloat16 [512, 8, 128, 128], P(('grp', 'seq'), 'head'), parts along dimension 0, may hold values from -5 to 5
- cache_values: bfloat16 [512, 8, 128, 128], P(('grp', 'seq'), 'head'), parts along dimension 0, may hold values from -6 to 6
- page_table: int32 [512], P('grp'), parts along dimension 0, may hold values from 0 to 255, as said below
- seq_lengths: int32 [16], P('grp'), parts along dimension 0, may hold values from 128 to 4096, as said below
Outputs:
- attended: bfloat16 [16, 32, 128], P('grp', 'head'), parts along dimension 0
There are 2 independent parts, one for each index of `grp`. A program takes and returns all parts, laid end to end along the dimension named above; each array names one. Nothing has to cross between parts.
Inputs may be any that keep to these rules, and one draw needn't show every extreme that they name: `page_table`: entry b * 32 + j is the pool slot of page j of sequence b; slot s lies on index s // 32 of seq; every slot appears once. `seq_lengths`: some sequence has exactly 4096 tokens.
All inputs are finite; a program needn't handle non-finite values.
Results may differ from a plain program's by a relative error of at most 0.0029.
Values may be sent and summed in bfloat16 or wider, within the bound.
A program may use at most 64 MiB of HBM per device.

v0:
```python
import math

import jax
import jax.numpy as jnp
from jax import lax
from jax.sharding import PartitionSpec as P

very_low = -1e30


def shards(query_rows, cache_keys, cache_values, page_table, seq_lengths):
    slot_count, kv_local, page_len, head_dim = cache_keys.shape
    batch_size, heads_local, _ = query_rows.shape
    group_size = heads_local // kv_local
    pool_size = page_table.shape[0]
    table_width = pool_size // batch_size
    score_scale = 1.0 / math.sqrt(head_dim)
    first_slot = lax.axis_index("seq") * slot_count
    slot_ids = first_slot + jnp.arange(slot_count, dtype=jnp.int32)
    matches = page_table[:, None] == slot_ids[None, :]
    entries = jnp.sum(
        jnp.where(matches, jnp.arange(pool_size, dtype=jnp.int32)[:, None], 0), axis=0
    )
    owners = entries // table_width
    logical = entries % table_width
    owner_hot = owners[:, None] == jnp.arange(batch_size, dtype=jnp.int32)[None, :]
    seq_len = jnp.sum(jnp.where(owner_hot, seq_lengths[None, :], 0), axis=1)
    positions = logical[:, None] * page_len + jnp.arange(page_len, dtype=jnp.int32)[None, :]
    live_mask = (positions < seq_len[:, None])[:, None, None, :]
    slot_query = jnp.take(query_rows, owners, axis=0).reshape(
        slot_count, kv_local, group_size, head_dim
    )
    scores = (
        jnp.einsum("sgqd,sgtd->sgqt", slot_query, cache_keys, preferred_element_type=jnp.float32)
        * score_scale
    )
    slot_top = jnp.max(jnp.where(live_mask, scores, very_low), axis=-1)
    local_top = jnp.max(jnp.where(owner_hot[:, :, None, None], slot_top[:, None], very_low), axis=0)
    row_top = lax.pmax(local_top.reshape(batch_size, heads_local), "seq")
    slot_ref = jnp.take(row_top, owners, axis=0).reshape(slot_count, kv_local, group_size)
    weights = jnp.where(live_mask, jnp.exp(scores - slot_ref[..., None]), 0.0)
    slot_total = jnp.sum(weights, axis=-1).reshape(slot_count, heads_local)
    slot_numer = jnp.einsum(
        "sgqt,sgtd->sgqd",
        weights.astype(jnp.bfloat16),
        cache_values,
        preferred_element_type=jnp.float32,
    ).reshape(slot_count, heads_local, head_dim)
    owner_float = owner_hot.astype(jnp.float32)
    totals = jnp.einsum(
        "sb,sr->br", owner_float, slot_total, precision=lax.Precision.HIGHEST
    ).reshape(batch_size * heads_local)
    numerators = jnp.einsum(
        "sb,srd->brd", owner_float, slot_numer, precision=lax.Precision.HIGHEST
    ).reshape(batch_size * heads_local, head_dim)
    summed_numer, summed_total = lax.psum((numerators, totals), "seq")
    finished = (summed_numer / summed_total[:, None]).astype(jnp.bfloat16)
    return finished.reshape(batch_size, heads_local, head_dim)


def solution(mesh):
    in_specs = (
        P("grp", "head", None),
        P(("grp", "seq"), "head", None, None),
        P(("grp", "seq"), "head", None, None),
        P("grp"),
        P("grp"),
    )
    out_specs = P("grp", "head", None)
    return jax.shard_map(shards, mesh=mesh, in_specs=in_specs, out_specs=out_specs, check_vma=False)
```

profile of v0, /device:TPU:0, one launch (start us, length us, event | category | flops | bytes accessed | tf_op | source)
XLA Modules:
  0.0 117.1 jit_solution(7496280859807679442)
XLA Ops:
  6.5 0.0 copy-start
  6.5 0.9 select_reduce_fusion.2
  7.5 0.7 select_reduce_fusion.3
  8.2 0.1 add_compare_fusion
  8.3 0.6 gather_fusion
  8.9 4.6 %select_reduce_fusion = (f32[32,4,4]{2,1,0:T(4,128)S(1)}, f32[32,4,4,128]{3,2,1,0:T(4,128)S(1)}) fusion(pred[32,128]{1,0:T(8,128)(4,1)S(1)} %add_compare_fusion, bf16[32,4,128,128]{3,2,1,0:T(8,128)(2,1)} %param.6, bf16[32,4,4,128]{3,2,1,0:T(4,128)(2,1)S(1)} %bitcast.25, pred[32]{0:T(512)(128)(4,1)S(1)} %get-tuple-element.5), kind=kOutput, calls=%fused_computation.6 | convolution fusion | flops 17038848 | bytes 4593696 | tf_op jit(solution)/shard_map/sgqd,sgtd->sgqt/dot_general | solution.py:34
  13.5 0.1 copy.28
  13.6 0.1 select_reduce_fusion.1
  13.7 0.1 copy.29
  13.8 23.1 %pmax.7 = f32[8,16]{1,0:T(8,128)S(1)} all-reduce(f32[8,16]{1,0:T(8,128)S(1)} %copy.29), channel_id=1, replica_groups=mesh['grp'=2,'seq'=8,'head'=2] {'seq'}, use_global_device_ids=true, to_apply=%region_4.5 | all-reduce | flops 128 | bytes 1024 | tf_op jit(solution)/shard_map/pmax | solution.py:39
  36.9 0.6 gather_fusion.1
  37.5 0.1 copy.30
  37.5 0.1 copy.31
  37.7 3.4 %fusion.4 = f32[32,4,4,128]{3,2,1,0:T(4,128)S(1)} fusion(bf16[32,4,128,128]{3,2,1,0:T(8,128)(2,1)} %param.7, f32[32,4,4,128]{3,2,1,0:T(4,128)S(1)} %get-tuple-element.8, f32[32,4,4]{2,1,0:T(4,128)S(1)} %copy.31, pred[32,128]{1,0:T(8,128)(4,1)S(1)} %add_compare_fusion), kind=kOutput, calls=%fused_computation.9 | convolution fusion | flops 16973824 | bytes 4724736 | tf_op jit(solution)/shard_map/sgqt,sgtd->sgqd/dot_general | solution.py:43
  41.1 0.3 fusion
  41.4 0.6 copy.33
  42.0 0.0 all-reduce.2.cloned.1.call-update
  42.1 0.4 fusion.2
  42.5 0.1 copy.34
  42.6 0.1 fusion.13
  42.7 0.1 reshape.170
  42.8 17.1 %psum.15 = f32[128]{0:T(128)S(1)} all-reduce(f32[128]{0:T(128)S(1)} %reshape.170), channel_id=1, replica_groups=mesh['grp'=2,'seq'=8,'head'=2] {'seq'}, use_global_device_ids=true, to_apply=%region_7.8 | all-reduce | flops 128 | bytes 1024 | tf_op jit(solution)/shard_map/psum | solution.py:56
  60.0 48.8 %all-reduce.2.cloned.1.call-done = f32[128,128]{1,0:T(8,128)} async-done(((f32[128,128]{1,0:T(8,128)}), f32[128,128]{1,0:T(8,128)}) %all-reduce.2.cloned.1.call-update) | async-done | bytes 65552 | tf_op jit(solution)/shard_map/psum | solution.py:56
  108.8 1.5 %divide_convert_fusion = bf16[128,128]{1,0:T(8,128)(2,1)} fusion(f32[128,128]{1,0:T(8,128)} %all-reduce.2.cloned.1.call-done, f32[128]{0:T(128)S(1)} %psum.15), kind=kLoop, calls=%fused_computation.15 | loop fusion | flops 32768 | bytes 98816 | tf_op jit(solution)/shard_map/convert_element_type | solution.py:57
  (9 shorter events, 0.1 us)
Async XLA Ops:
  6.5 1.8 %copy-start = (bf16[8,16,128]{2,1,0:T(8,128)(2,1)S(1)}, bf16[8,16,128]{2,1,0:T(8,128)(2,1)}, u32[]{:S(2)}) copy-start(bf16[8,16,128]{2,1,0:T(8,128)(2,1)} %param.5) | copy-start | bytes 98308
  6.5 102.2 %all-reduce.2.cloned.1.call-start = ((), (), s32[]{:S(2)}) async-start(), calls=%async_computation | async-start | bytes 131072 | tf_op jit(solution)/shard_map/psum | solution.py:56
Sparse Core Ops, SparseCore 0:
  42.2 66.5 all-reduce.1
where the time goes:
time: 117 us
  waiting for transfers between devices  48.8 us (42%)
  blocking collectives  40.3 us (34%)
  between operations  13.4 us (11%)
  matrix products  8.45 us (7%)
  other arithmetic  3.83 us (3%)
  local copies, waits for them, and re-layouts  2.33 us (2%)
    psum x1, waiting for transfers between devices, shards(): summed_numer, summed_total = lax.psum((numerators, totals), 'seq')  48.8 us
    pmax x1, blocking collectives, shards(): row_top = lax.pmax(local_top.reshape(batch_size, heads_local), 'seq')  23.1 us
    psum x1, blocking collectives, shards(): summed_numer, summed_total = lax.psum((numerators, totals), 'seq')  17.1 us
    dot_general x1, matrix products, shards(): jnp.einsum('sgqd,sgtd->sgqt', slot_query, cache_keys, preferred_element_t...  4.6 us
    dot_general x1, matrix products, shards(): jnp.einsum('sgqt,sgtd->sgqd', weights.astype(jnp.bfloat16), cache_values,...  3.45 us
  transfers between devices with their start and end apart: 1, of which 1 were waited for; matrix products, arithmetic and copies ran while one was open for 1% of the time, Pallas kernels for 0%

commit v1 on v0

v1 whole, which is shorter than its diff:
```python
import functools
import math

import jax
import jax.numpy as jnp
from jax import lax
from jax.experimental import pallas as pl
from jax.experimental.pallas import tpu as pltpu
from jax.sharding import PartitionSpec as P

MESH = pl.DeviceIdType.MESH
VERY_LOW = -1e30
FLOOR = -1e29


def attend(
    n,
    table_width,
    q_hbm,
    k_hbm,
    v_hbm,
    pt_hbm,
    len_hbm,
    out_ref,
    q_raw,
    q_rows,
    pt_vmem,
    len_smem,
    k_vmem,
    v_vmem,
    mask_ref,
    stat_out,
    stat_in,
    num_out,
    num_in,
    small_sem,
    k_sem,
    v_sem,
    stat_send,
    stat_recv,
    num_send,
    num_recv,
    fin_send,
    fin_recv,
):
    me = lax.axis_index("seq")
    batch, heads, head_dim = q_raw.shape
    kv_heads, slots, page, _ = k_vmem.shape
    group = heads // kv_heads
    rows = group * batch
    per_dev = out_ref.shape[1]
    pool = pt_vmem.shape[0]

    small = (
        pltpu.make_async_copy(q_hbm, q_raw, small_sem.at[0]),
        pltpu.make_async_copy(pt_hbm, pt_vmem, small_sem.at[1]),
        pltpu.make_async_copy(len_hbm, len_smem, small_sem.at[2]),
    )
    for copy in small:
        copy.start()
    k_copies, v_copies = [], []
    for g in range(kv_heads):
        k_copies.append(pltpu.make_async_copy(k_hbm.at[:, g], k_vmem.at[g], k_sem.at[g]))
        v_copies.append(pltpu.make_async_copy(v_hbm.at[:, g], v_vmem.at[g], v_sem.at[g]))
        k_copies[g].start()
        v_copies[g].start()

    barrier = pltpu.get_barrier_semaphore()
    for step in range(1, n):
        pl.semaphore_signal(
            barrier, inc=1, device_id={"seq": lax.rem(me + step, n)}, device_id_type=MESH
        )

    for copy in small:
        copy.wait()

    q_rows[...] = q_raw[...].astype(jnp.float32).reshape(batch * heads, head_dim)

    entry = lax.broadcasted_iota(jnp.int32, (1, pool), 1)
    span = 8 * page
    code = jnp.zeros((1, pool), jnp.int32)
    for b in range(batch):
        live = jnp.clip(len_smem[b] - page * (entry - b * table_width), 0, page)
        code = jnp.where(entry >= b * table_width, b * span + live, code)
    slot_ids = me * slots + lax.broadcasted_iota(jnp.int32, (slots, pool), 0)
    hit = pt_vmem[...].reshape(1, pool) == slot_ids
    slot_code = jnp.sum(
        jnp.where(hit, code.astype(jnp.float32), 0.0), axis=1, keepdims=True
    )
    slot_code = jnp.broadcast_to(slot_code, (slots, page))
    base = (lax.broadcasted_iota(jnp.int32, (batch, page), 0) * span).astype(jnp.float32)
    token = lax.broadcasted_iota(jnp.int32, (batch, page), 1).astype(jnp.float32)
    for s in range(slots):
        left = slot_code[s : s + 1, :] - base
        live = (token < left) & (left <= float(page))
        mask_ref[:, s * page : (s + 1) * page] = jnp.where(live, 0.0, VERY_LOW)

    factor = math.log2(math.e) / math.sqrt(head_dim)
    half = lax.broadcasted_iota(jnp.int32, (rows, head_dim), 1) < head_dim // 2
    per_group = rows // per_dev

    def stat_copy(dest, slot):
        return pltpu.make_async_remote_copy(
            src_ref=stat_out.at[dest],
            dst_ref=stat_in.at[slot],
            send_sem=stat_send.at[dest],
            recv_sem=stat_recv.at[slot],
            device_id={"seq": dest},
            device_id_type=MESH,
        )

    def num_copy(dest, slot):
        return pltpu.make_async_remote_copy(
            src_ref=num_out.at[dest],
            dst_ref=num_in.at[slot],
            send_sem=num_send.at[dest],
            recv_sem=num_recv.at[slot],
            device_id={"seq": dest},
            device_id_type=MESH,
        )

    def fin_copy(dest, slot):
        return pltpu.make_async_remote_copy(
            src_ref=out_ref.at[slot],
            dst_ref=out_ref.at[slot],
            send_sem=fin_send.at[dest],
            recv_sem=fin_recv.at[slot],
            device_id={"seq": dest},
            device_id_type=MESH,
        )

    def send(make, dest):
        @pl.when(dest != me)
        def _():
            make(dest, me).start()

    for g in range(kv_heads):
        q_g = jnp.concatenate(
            [q_rows[pl.ds(g * group + h, batch, stride=heads), :] for h in range(group)], axis=0
        ).astype(jnp.bfloat16)
        k_copies[g].wait()
        scores = lax.dot_general(
            q_g,
            k_vmem[g].reshape(slots * page, head_dim),
            (((1,), (1,)), ((), ())),
            preferred_element_type=jnp.float32,
        )
        scores = scores + jnp.concatenate([mask_ref[...]] * group, axis=0)
        top = jnp.maximum(jnp.max(scores, axis=1, keepdims=True), FLOOR)
        weights = jnp.exp2((scores - top) * factor)
        total = jnp.sum(weights, axis=1, keepdims=True)
        stats = jnp.where(half, top, total)
        if g == 0:
            pl.semaphore_wait(barrier, n - 1)
        for i in range(per_group):
            dest = g * per_group + i
            stat_out[dest] = stats[i * per_dev : (i + 1) * per_dev]
            send(stat_copy, dest)
        high = weights.astype(jnp.bfloat16)
        low = (weights - high.astype(jnp.float32)).astype(jnp.bfloat16)
        v_copies[g].wait()
        numer = jnp.dot(
            jnp.concatenate([high, low], axis=0),
            v_vmem[g].reshape(slots * page, head_dim),
            preferred_element_type=jnp.float32,
        )
        numer = numer[:rows] + numer[rows:]
        for i in range(per_group):
            dest = g * per_group + i
            num_out[dest] = numer[i * per_dev : (i + 1) * per_dev]
            send(num_copy, dest)

    stat_in[me] = stat_out[me]
    num_in[me] = num_out[me]
    for step in range(1, n):
        stat_copy(0, lax.rem(me + step, n)).wait_recv()
    tops, totals = [], []
    for s in range(n):
        stat = stat_in[s]
        tops.append(stat[:, :1])
        totals.append(stat[:, head_dim // 2 : head_dim // 2 + 1])
    best = functools.reduce(jnp.maximum, tops)
    scales = [jnp.exp2((top - best) * factor) for top in tops]
    inverse = 1.0 / sum(scale * total for scale, total in zip(scales, totals))
    scales = [scale * inverse for scale in scales]
    for step in range(1, n):
        num_copy(0, lax.rem(me + step, n)).wait_recv()
    result = sum(scales[s] * num_in[s] for s in range(n))
    out_ref[me] = result.astype(out_ref.dtype)
    for step in range(1, n):
        fin_copy(lax.rem(me + step, n), me).start()
    for dest in range(n):
        @pl.when(dest != me)
        def _():
            stat_copy(dest, me).wait_send()
            num_copy(dest, me).wait_send()
    for step in range(1, n):
        fin_copy(0, lax.rem(me + step, n)).wait_recv()
    for step in range(1, n):
        fin_copy(lax.rem(me + step, n), me).wait_send()


def shards(n, query_rows, cache_keys, cache_values, page_table, seq_lengths):
    slots, kv_heads, page, head_dim = cache_keys.shape
    batch, heads, _ = query_rows.shape
    pool = page_table.shape[0]
    per_dev = batch * heads // n
    f32, bf16 = jnp.float32, jnp.bfloat16
    hbm = pl.BlockSpec(memory_space=pl.ANY)
    out = pl.pallas_call(
        functools.partial(attend, n, pool // batch),
        out_shape=jax.ShapeDtypeStruct((n, per_dev, head_dim), bf16),
        in_specs=[hbm] * 5,
        out_specs=pl.BlockSpec(memory_space=pltpu.VMEM),
        scratch_shapes=[
            pltpu.VMEM((batch, heads, head_dim), bf16),
            pltpu.VMEM((batch * heads, head_dim), f32),
            pltpu.VMEM((pool,), jnp.int32),
            pltpu.SMEM((batch,), jnp.int32),
            pltpu.VMEM((kv_heads, slots, page, head_dim), bf16),
            pltpu.VMEM((kv_heads, slots, page, head_dim), bf16),
            pltpu.VMEM((batch, slots * page), f32),
            pltpu.VMEM((n, per_dev, head_dim), f32),
            pltpu.VMEM((n, per_dev, head_dim), f32),
            pltpu.VMEM((n, per_dev, head_dim), f32),
            pltpu.VMEM((n, per_dev, head_dim), f32),
            pltpu.SemaphoreType.DMA((3,)),
            pltpu.SemaphoreType.DMA((kv_heads,)),
            pltpu.SemaphoreType.DMA((kv_heads,)),
        ]
        + [pltpu.SemaphoreType.DMA((n,))] * 6,
        compiler_params=pltpu.CompilerParams(collective_id=0, has_side_effects=True),
    )(query_rows, cache_keys, cache_values, page_table, seq_lengths)
    return out.reshape(heads, batch, head_dim).transpose(1, 0, 2)


def solution(mesh):
    in_specs = (
        P("grp", "head", None),
        P(("grp", "seq"), "head", None, None),
        P(("grp", "seq"), "head", None, None),
        P("grp"),
        P("grp"),
    )
    return jax.shard_map(
        functools.partial(shards, mesh.shape["seq"]),
        mesh=mesh,
        in_specs=in_specs,
        out_specs=P("grp", "head", None),
        check_vma=False,
    )
```

time: 117 us -> 20.4 us (0.17)
  waiting for transfers between devices: 48.8 us -> 0 us
  blocking collectives: 40.3 us -> 0 us
  Pallas kernels: 0 us -> 18.9 us
  between operations: 13.4 us -> 0.01 us
  matrix products: 8.45 us -> 0 us
  other arithmetic: 3.83 us -> 0 us
    psum x1 -> x0, waiting for transfers between devices: 48.8 us -> none  [shards(): summed_numer, summed_total = lax.psum((numerators, totals), 'seq')]
    pmax x1 -> x0, blocking collectives: 23.1 us -> none  [shards(): row_top = lax.pmax(local_top.reshape(batch_size, heads_local), 'seq')]
    pallas_call x0 -> x1, Pallas kernels: none -> 18.9 us  [shards(): pl.pallas_call(functools.partial(attend, n, pool // batch), out_shape=jax...]
    psum x1 -> x0, blocking collectives: 17.1 us -> none  [shards(): summed_numer, summed_total = lax.psum((numerators, totals), 'seq')]
    dot_general x4 -> x0, matrix products: 8.45 us -> none  [the longest x1 4.6 us: shards(): jnp.einsum('sgqd,sgtd->sgqt', slot_query, cache_keys, preferred_element_t...]
    reduce_sum x3 -> x0, other arithmetic: 2.05 us -> none  [the longest x1 0.86 us: shards(): jnp.sum(jnp.where(matches, jnp.arange(pool_size, dtype=jnp.int32)[:, None...]
    convert_element_type x1 -> x0, other arithmetic: 1.54 us -> none  [shards(): finished = (summed_numer / summed_total[:, None]).astype(jnp.bfloat16)]
    gather x3 -> x0, local copies, waits for them, and re-layouts: 1.23 us -> none  [the longest x2 0.64 us: shards(): jnp.take(row_top, owners, axis=0).reshape(slot_count, kv_local, group_size)]
  transfers between devices with their start and end apart: 1 -> 0, of which waited for: 1 -> 0; matrix products, arithmetic and copies ran while one was open for 1% -> 0% of each run, Pallas kernels for 0% -> 0%
where the time goes in v1:
time: 20.4 us; the launch traced here: 20.2 us
  Pallas kernels  18.9 us (93%)
  local copies, waits for them, and re-layouts  1.38 us (7%)
    pallas_call x1, Pallas kernels, shards(): pl.pallas_call(functools.partial(attend, n, pool // batch), out_shape=jax...  18.9 us
    reshape x1, local copies, waits for them, and re-layouts, shards(): return out.reshape(heads, batch, head_dim).transpose(1, 0, 2)  1.38 us

profile of v1, /device:TPU:0, one launch (start us, length us, event | category | flops | bytes accessed | tf_op | source)
XLA Modules:
  0.0 20.2 jit_solution(11881471061670207855)
XLA Ops:
  0.0 18.9 %shard_map.55 = bf16[8,16,128]{2,1,0:T(8,128)(2,1)} custom-call(bf16[8,16,128]{2,1,0:T(8,128)(2,1)} %q_hbm.1, bf16[32,4,128,128]{3,2,1,0:T(8,128)(2,1)} %k_hbm.1, bf16[32,4,128,128]{3,2,1,0:T(8,128)(2,1)} %v_hbm.1, s32[256]{0:T(256)} %pt_hbm.1, s32[8]{0:T(128)} %len_hbm.1), custom_call_target="tpu_custom_call" | custom-call | tf_op jit(solution)/shard_map/pallas_call | solution.py:210
  18.9 1.4 %copy.8 = bf16[16,8,128]{2,0,1:T(8,128)(2,1)} copy(bf16[16,8,128]{2,1,0:T(8,128)(2,1)} %bitcast.4) | data formatting | bytes 65536 | tf_op jit(solution)/shard_map/reshape | solution.py:234

commit v2 on v1

--- a/solution.py
+++ b/solution.py
@@ -62,8 +62,11 @@
     for g in range(kv_heads):
         k_copies.append(pltpu.make_async_copy(k_hbm.at[:, g], k_vmem.at[g], k_sem.at[g]))
         v_copies.append(pltpu.make_async_copy(v_hbm.at[:, g], v_vmem.at[g], v_sem.at[g]))
-        k_copies[g].start()
-        v_copies[g].start()
+
+    order = [(k_copies, g, 2 * g) for g in range(kv_heads)]
+    order += [(v_copies, g, 2 * g + 3) for g in range(kv_heads)]
+    for copies, g, _ in sorted(order, key=lambda item: item[2]):
+        copies[g].start()
 
     barrier = pltpu.get_barrier_semaphore()
     for step in range(1, n):
@@ -134,41 +137,58 @@
         def _():
             make(dest, me).start()
 
-    for g in range(kv_heads):
+    def score(g):
         q_g = jnp.concatenate(
             [q_rows[pl.ds(g * group + h, batch, stride=heads), :] for h in range(group)], axis=0
         ).astype(jnp.bfloat16)
-        k_copies[g].wait()
-        scores = lax.dot_general(
+        return lax.dot_general(
             q_g,
             k_vmem[g].reshape(slots * page, head_dim),
             (((1,), (1,)), ((), ())),
             preferred_element_type=jnp.float32,
         )
+
+    def soften(scores):
         scores = scores + jnp.concatenate([mask_ref[...]] * group, axis=0)
         top = jnp.maximum(jnp.max(scores, axis=1, keepdims=True), FLOOR)
         weights = jnp.exp2((scores - top) * factor)
         total = jnp.sum(weights, axis=1, keepdims=True)
-        stats = jnp.where(half, top, total)
-        if g == 0:
-            pl.semaphore_wait(barrier, n - 1)
+        high = weights.astype(jnp.bfloat16)
+        low = (weights - high.astype(jnp.float32)).astype(jnp.bfloat16)
+        return jnp.where(half, top, total), jnp.concatenate([high, low], axis=0)
+
+    def gather(g, weights):
+        numer = jnp.dot(
+            weights,
+            v_vmem[g].reshape(slots * page, head_dim),
+            preferred_element_type=jnp.float32,
+        )
+        return numer[:rows] + numer[rows:]
+
+    def send_all(make, buffer, g, value):
         for i in range(per_group):
             dest = g * per_group + i
-            stat_out[dest] = stats[i * per_dev : (i + 1) * per_dev]
-            send(stat_copy, dest)
-        high = weights.astype(jnp.bfloat16)
-        low = (weights - high.astype(jnp.float32)).astype(jnp.bfloat16)
-        v_copies[g].wait()
-        numer = jnp.dot(
-            jnp.concatenate([high, low], axis=0),
-            v_vmem[g].reshape(slots * page, head_dim),
-            preferred_element_type=jnp.float32,
-        )
-        numer = numer[:rows] + numer[rows:]
-        for i in range(per_group):
-            dest = g * per_group + i
-            num_out[dest] = numer[i * per_dev : (i + 1) * per_dev]
-            send(num_copy, dest)
+            buffer[dest] = value[i * per_dev : (i + 1) * per_dev]
+            send(make, dest)
+
+    scores, weights = {}, {}
+    for t in range(kv_heads + 2):
+        if t < kv_heads:
+            k_copies[t].wait()
+        if t >= 2:
+            v_copies[t - 2].wait()
+        if t < kv_heads:
+            scores[t] = score(t)
+        if 1 <= t <= kv_heads:
+            stats, weights[t - 1] = soften(scores.pop(t - 1))
+        if t >= 2:
+            numer = gather(t - 2, weights.pop(t - 2))
+        if t == 1:
+            pl.semaphore_wait(barrier, n - 1)
+        if 1 <= t <= kv_heads:
+            send_all(stat_copy, stat_out, t - 1, stats)
+        if t >= 2:
+            send_all(num_copy, num_out, t - 2, numer)
 
     stat_in[me] = stat_out[me]
     num_in[me] = num_out[me]
@@ -209,7 +229,7 @@
     hbm = pl.BlockSpec(memory_space=pl.ANY)
     out = pl.pallas_call(
         functools.partial(attend, n, pool // batch),
-        out_shape=jax.ShapeDtypeStruct((n, per_dev, head_dim), bf16),
+        out_shape=pltpu.VMEM((n, per_dev, head_dim), bf16),
         in_specs=[hbm] * 5,
         out_specs=pl.BlockSpec(memory_space=pltpu.VMEM),
         scratch_shapes=[

time: 20.4 us -> 18.6 us (0.912)
  Pallas kernels: 18.9 us -> 17.8 us
  local copies, waits for them, and re-layouts: 1.38 us -> 0.62 us
    pallas_call x1, Pallas kernels: 18.9 us -> 17.8 us  [shards(): pl.pallas_call(functools.partial(attend, n, pool // batch), out_shape=plt...]
    reshape x1, local copies, waits for them, and re-layouts: 1.38 us -> 0.62 us  [shards(): return out.reshape(heads, batch, head_dim).transpose(1, 0, 2)]
where the time goes in v2:
time: 18.6 us; the launch traced here: 18.4 us
  Pallas kernels  17.8 us (96%)
  local copies, waits for them, and re-layouts  0.62 us (3%)
    pallas_call x1, Pallas kernels, shards(): pl.pallas_call(functools.partial(attend, n, pool // batch), out_shape=plt...  17.8 us
    reshape x1, local copies, waits for them, and re-layouts, shards(): return out.reshape(heads, batch, head_dim).transpose(1, 0, 2)  0.62 us

profile of v2, /device:TPU:0, one launch (start us, length us, event | category | flops | bytes accessed | tf_op | source)
XLA Modules:
  0.0 18.4 jit_solution(13837037139307249326)
XLA Ops:
  0.0 17.8 %shard_map.55 = bf16[8,16,128]{2,1,0:T(8,128)(2,1)S(1)} custom-call(bf16[8,16,128]{2,1,0:T(8,128)(2,1)} %q_hbm.1, bf16[32,4,128,128]{3,2,1,0:T(8,128)(2,1)} %k_hbm.1, bf16[32,4,128,128]{3,2,1,0:T(8,128)(2,1)} %v_hbm.1, s32[256]{0:T(256)} %pt_hbm.1, s32[8]{0:T(128)} %len_hbm.1), custom_call_target="tpu_custom_call" | custom-call | tf_op jit(solution)/shard_map/pallas_call | solution.py:230
  17.8 0.6 %copy.8 = bf16[16,8,128]{2,0,1:T(8,128)(2,1)} copy(bf16[16,8,128]{2,1,0:T(8,128)(2,1)S(1)} %bitcast.4) | data formatting | bytes 65536 | tf_op jit(solution)/shard_map/reshape | solution.py:254

commit v3 on v2

--- a/solution.py
+++ b/solution.py
@@ -76,6 +76,7 @@
 
     for copy in small:
         copy.wait()
+    stat_out[...] = jnp.zeros_like(stat_out)
 
     q_rows[...] = q_raw[...].astype(jnp.float32).reshape(batch * heads, head_dim)
 
@@ -155,7 +156,9 @@
         total = jnp.sum(weights, axis=1, keepdims=True)
         high = weights.astype(jnp.bfloat16)
         low = (weights - high.astype(jnp.float32)).astype(jnp.bfloat16)
-        return jnp.where(half, top, total), jnp.concatenate([high, low], axis=0)
+        stats = jnp.where(half, top, total).T
+        stats = (stats[:1], stats[head_dim // 2 : head_dim // 2 + 1])
+        return stats, jnp.concatenate([high, low], axis=0)
 
     def gather(g, weights):
         numer = jnp.dot(
@@ -165,13 +168,23 @@
         )
         return numer[:rows] + numer[rows:]
 
-    def send_all(make, buffer, g, value):
+    def post_stats(g, stats):
         for i in range(per_group):
             dest = g * per_group + i
-            buffer[dest] = value[i * per_dev : (i + 1) * per_dev]
-            send(make, dest)
-
-    scores, weights = {}, {}
+            for row in range(2):
+                stat_out[dest, row : row + 1, :per_dev] = stats[row][
+                    :, i * per_dev : (i + 1) * per_dev
+                ]
+            waiting.append((stat_copy, dest))
+
+    def post_numer(g, numer):
+        for i in range(per_group):
+            dest = g * per_group + i
+            num_out[dest] = numer[i * per_dev : (i + 1) * per_dev]
+            waiting.append((num_copy, dest))
+
+    scores, weights, waiting = {}, {}, []
+    opening = kv_heads + -1
     for t in range(kv_heads + 2):
         if t < kv_heads:
             k_copies[t].wait()
@@ -183,26 +196,25 @@
             stats, weights[t - 1] = soften(scores.pop(t - 1))
         if t >= 2:
             numer = gather(t - 2, weights.pop(t - 2))
-        if t == 1:
+        if 1 <= t <= kv_heads:
+            post_stats(t - 1, stats)
+        if t >= 2:
+            post_numer(t - 2, numer)
+        if t == opening:
             pl.semaphore_wait(barrier, n - 1)
-        if 1 <= t <= kv_heads:
-            send_all(stat_copy, stat_out, t - 1, stats)
-        if t >= 2:
-            send_all(num_copy, num_out, t - 2, numer)
+        if t >= opening:
+            for make, dest in waiting:
+                send(make, dest)
+            waiting = []
 
     stat_in[me] = stat_out[me]
     num_in[me] = num_out[me]
     for step in range(1, n):
         stat_copy(0, lax.rem(me + step, n)).wait_recv()
-    tops, totals = [], []
-    for s in range(n):
-        stat = stat_in[s]
-        tops.append(stat[:, :1])
-        totals.append(stat[:, head_dim // 2 : head_dim // 2 + 1])
-    best = functools.reduce(jnp.maximum, tops)
-    scales = [jnp.exp2((top - best) * factor) for top in tops]
-    inverse = 1.0 / sum(scale * total for scale, total in zip(scales, totals))
-    scales = [scale * inverse for scale in scales]
+    tops, totals = stat_in[:, 0, :], stat_in[:, 1, :]
+    scales = jnp.exp2((tops - jnp.max(tops, axis=0, keepdims=True)) * factor)
+    scales = (scales / jnp.sum(scales * totals, axis=0, keepdims=True)).T[:per_dev]
+    scales = [jnp.broadcast_to(scales[:, s : s + 1], (per_dev, head_dim)) for s in range(n)]
     for step in range(1, n):
         num_copy(0, lax.rem(me + step, n)).wait_recv()
     result = sum(scales[s] * num_in[s] for s in range(n))
@@ -240,8 +252,8 @@
             pltpu.VMEM((kv_heads, slots, page, head_dim), bf16),
             pltpu.VMEM((kv_heads, slots, page, head_dim), bf16),
             pltpu.VMEM((batch, slots * page), f32),
-            pltpu.VMEM((n, per_dev, head_dim), f32),
-            pltpu.VMEM((n, per_dev, head_dim), f32),
+            pltpu.VMEM((n, 2, head_dim), f32),
+            pltpu.VMEM((n, 2, head_dim), f32),
             pltpu.VMEM((n, per_dev, head_dim), f32),
             pltpu.VMEM((n, per_dev, head_dim), f32),
             pltpu.SemaphoreType.DMA((3,)),

time: 18.6 us -> 17.9 us (0.962)
  Pallas kernels: 17.8 us -> 17.1 us
    pallas_call x1, Pallas kernels: 17.8 us -> 17.1 us  [shards(): pl.pallas_call(functools.partial(attend, n, pool // batch), out_shape=plt...]
where the time goes in v3:
time: 17.9 us; the launch traced here: 17.7 us
  Pallas kernels  17.1 us (96%)
  local copies, waits for them, and re-layouts  0.62 us (3%)
    pallas_call x1, Pallas kernels, shards(): pl.pallas_call(functools.partial(attend, n, pool // batch), out_shape=plt...  17.1 us
    reshape x1, local copies, waits for them, and re-layouts, shards(): return out.reshape(heads, batch, head_dim).transpose(1, 0, 2)  0.62 us

profile of v3, /device:TPU:0, one launch (start us, length us, event | category | flops | bytes accessed | tf_op | source)
XLA Modules:
  0.0 17.7 jit_solution(320647779800508161)
XLA Ops:
  0.0 17.1 %shard_map.55 = bf16[8,16,128]{2,1,0:T(8,128)(2,1)S(1)} custom-call(bf16[8,16,128]{2,1,0:T(8,128)(2,1)} %q_hbm.1, bf16[32,4,128,128]{3,2,1,0:T(8,128)(2,1)} %k_hbm.1, bf16[32,4,128,128]{3,2,1,0:T(8,128)(2,1)} %v_hbm.1, s32[256]{0:T(256)} %pt_hbm.1, s32[8]{0:T(128)} %len_hbm.1), custom_call_target="tpu_custom_call" | custom-call | tf_op jit(solution)/shard_map/pallas_call | solution.py:242
  17.1 0.6 %copy.8 = bf16[16,8,128]{2,0,1:T(8,128)(2,1)} copy(bf16[16,8,128]{2,1,0:T(8,128)(2,1)S(1)} %bitcast.4) | data formatting | bytes 65536 | tf_op jit(solution)/shard_map/reshape | solution.py:266

commit v4 on v3

--- a/solution.py
+++ b/solution.py
@@ -74,30 +74,10 @@
             barrier, inc=1, device_id={"seq": lax.rem(me + step, n)}, device_id_type=MESH
         )
 
-    for copy in small:
-        copy.wait()
+    small[0].wait()
     stat_out[...] = jnp.zeros_like(stat_out)
 
     q_rows[...] = q_raw[...].astype(jnp.float32).reshape(batch * heads, head_dim)
-
-    entry = lax.broadcasted_iota(jnp.int32, (1, pool), 1)
-    span = 8 * page
-    code = jnp.zeros((1, pool), jnp.int32)
-    for b in range(batch):
-        live = jnp.clip(len_smem[b] - page * (entry - b * table_width), 0, page)
-        code = jnp.where(entry >= b * table_width, b * span + live, code)
-    slot_ids = me * slots + lax.broadcasted_iota(jnp.int32, (slots, pool), 0)
-    hit = pt_vmem[...].reshape(1, pool) == slot_ids
-    slot_code = jnp.sum(
-        jnp.where(hit, code.astype(jnp.float32), 0.0), axis=1, keepdims=True
-    )
-    slot_code = jnp.broadcast_to(slot_code, (slots, page))
-    base = (lax.broadcasted_iota(jnp.int32, (batch, page), 0) * span).astype(jnp.float32)
-    token = lax.broadcasted_iota(jnp.int32, (batch, page), 1).astype(jnp.float32)
-    for s in range(slots):
-        left = slot_code[s : s + 1, :] - base
-        live = (token < left) & (left <= float(page))
-        mask_ref[:, s * page : (s + 1) * page] = jnp.where(live, 0.0, VERY_LOW)
 
     factor = math.log2(math.e) / math.sqrt(head_dim)
     half = lax.broadcasted_iota(jnp.int32, (rows, head_dim), 1) < head_dim // 2
@@ -155,10 +135,9 @@
         weights = jnp.exp2((scores - top) * factor)
         total = jnp.sum(weights, axis=1, keepdims=True)
         high = weights.astype(jnp.bfloat16)
-        low = (weights - high.astype(jnp.float32)).astype(jnp.bfloat16)
         stats = jnp.where(half, top, total).T
         stats = (stats[:1], stats[head_dim // 2 : head_dim // 2 + 1])
-        return stats, jnp.concatenate([high, low], axis=0)
+        return stats, high
 
     def gather(g, weights):
         numer = jnp.dot(
@@ -166,7 +145,7 @@
             v_vmem[g].reshape(slots * page, head_dim),
             preferred_element_type=jnp.float32,
         )
-        return numer[:rows] + numer[rows:]
+        return numer
 
     def post_stats(g, stats):
         for i in range(per_group):
@@ -183,15 +162,40 @@
             num_out[dest] = numer[i * per_dev : (i + 1) * per_dev]
             waiting.append((num_copy, dest))
 
+    def build_mask():
+        entry = lax.broadcasted_iota(jnp.int32, (1, pool), 1)
+        span = 8 * page
+        code = jnp.zeros((1, pool), jnp.int32)
+        for b in range(batch):
+            live = jnp.clip(len_smem[b] - page * (entry - b * table_width), 0, page)
+            code = jnp.where(entry >= b * table_width, b * span + live, code)
+        slot_ids = me * slots + lax.broadcasted_iota(jnp.int32, (slots, pool), 0)
+        hit = pt_vmem[...].reshape(1, pool) == slot_ids
+        slot_code = jnp.sum(
+            jnp.where(hit, code.astype(jnp.float32), 0.0), axis=1, keepdims=True
+        )
+        slot_code = jnp.broadcast_to(slot_code, (slots, page))
+        base = (lax.broadcasted_iota(jnp.int32, (batch, page), 0) * span).astype(jnp.float32)
+        token = lax.broadcasted_iota(jnp.int32, (batch, page), 1).astype(jnp.float32)
+        for s in range(slots):
+            left = slot_code[s : s + 1, :] - base
+            live = (token < left) & (left <= float(page))
+            mask_ref[:, s * page : (s + 1) * page] = jnp.where(live, 0.0, VERY_LOW)
+
     scores, weights, waiting = {}, {}, []
     opening = kv_heads + -1
     for t in range(kv_heads + 2):
+        if t == 0:
+            small[1].wait()
+            small[2].wait()
         if t < kv_heads:
             k_copies[t].wait()
         if t >= 2:
             v_copies[t - 2].wait()
         if t < kv_heads:
             scores[t] = score(t)
+        if t == 0:
+            build_mask()
         if 1 <= t <= kv_heads:
             stats, weights[t - 1] = soften(scores.pop(t - 1))
         if t >= 2:

time: 17.9 us -> 17.4 us (0.972)
  Pallas kernels: 17.1 us -> 16.6 us
    pallas_call x1, Pallas kernels: 17.1 us -> 16.6 us  [shards(): pl.pallas_call(functools.partial(attend, n, pool // batch), out_shape=plt...]
where the time goes in v4:
time: 17.4 us; the launch traced here: 17.3 us
  Pallas kernels  16.6 us (95%)
  local copies, waits for them, and re-layouts  0.62 us (4%)
    pallas_call x1, Pallas kernels, shards(): pl.pallas_call(functools.partial(attend, n, pool // batch), out_shape=plt...  16.6 us
    reshape x1, local copies, waits for them, and re-layouts, shards(): return out.reshape(heads, batch, head_dim).transpose(1, 0, 2)  0.62 us

profile of v4, /device:TPU:0, one launch (start us, length us, event | category | flops | bytes accessed | tf_op | source)
XLA Modules:
  0.0 17.3 jit_solution(6613047234341544032)
XLA Ops:
  0.0 16.6 %shard_map.55 = bf16[8,16,128]{2,1,0:T(8,128)(2,1)S(1)} custom-call(bf16[8,16,128]{2,1,0:T(8,128)(2,1)} %q_hbm.1, bf16[32,4,128,128]{3,2,1,0:T(8,128)(2,1)} %k_hbm.1, bf16[32,4,128,128]{3,2,1,0:T(8,128)(2,1)} %v_hbm.1, s32[256]{0:T(256)} %pt_hbm.1, s32[8]{0:T(128)} %len_hbm.1), custom_call_target="tpu_custom_call" | custom-call | tf_op jit(solution)/shard_map/pallas_call | solution.py:246
  16.6 0.6 %copy.8 = bf16[16,8,128]{2,0,1:T(8,128)(2,1)} copy(bf16[16,8,128]{2,1,0:T(8,128)(2,1)S(1)} %bitcast.4) | data formatting | bytes 65536 | tf_op jit(solution)/shard_map/reshape | solution.py:270

commit v5 on v4

--- a/solution.py
+++ b/solution.py
@@ -135,9 +135,7 @@
         weights = jnp.exp2((scores - top) * factor)
         total = jnp.sum(weights, axis=1, keepdims=True)
         high = weights.astype(jnp.bfloat16)
-        stats = jnp.where(half, top, total).T
-        stats = (stats[:1], stats[head_dim // 2 : head_dim // 2 + 1])
-        return stats, high
+        return jnp.where(half, top, total), high
 
     def gather(g, weights):
         numer = jnp.dot(
@@ -147,12 +145,13 @@
         )
         return numer
 
-    def post_stats(g, stats):
-        for i in range(per_group):
-            dest = g * per_group + i
+    def post_stats(stats):
+        stats = jnp.concatenate(stats, axis=0).T
+        for dest in range(n):
             for row in range(2):
-                stat_out[dest, row : row + 1, :per_dev] = stats[row][
-                    :, i * per_dev : (i + 1) * per_dev
+                line = row * (head_dim // 2)
+                stat_out[dest, row : row + 1, :per_dev] = stats[
+                    line : line + 1, dest * per_dev : (dest + 1) * per_dev
                 ]
             waiting.append((stat_copy, dest))
 
@@ -182,7 +181,7 @@
             live = (token < left) & (left <= float(page))
             mask_ref[:, s * page : (s + 1) * page] = jnp.where(live, 0.0, VERY_LOW)
 
-    scores, weights, waiting = {}, {}, []
+    scores, weights, stats, waiting = {}, {}, [], []
     opening = kv_heads + -1
     for t in range(kv_heads + 2):
         if t == 0:
@@ -197,11 +196,12 @@
         if t == 0:
             build_mask()
         if 1 <= t <= kv_heads:
-            stats, weights[t - 1] = soften(scores.pop(t - 1))
+            tops_here, weights[t - 1] = soften(scores.pop(t - 1))
+            stats.append(tops_here)
         if t >= 2:
             numer = gather(t - 2, weights.pop(t - 2))
-        if 1 <= t <= kv_heads:
-            post_stats(t - 1, stats)
+        if t == kv_heads:
+            post_stats(stats)
         if t >= 2:
             post_numer(t - 2, numer)
         if t == opening:

time: 17.4 us -> 17 us (0.977)
  Pallas kernels: 16.6 us -> 16.2 us
    pallas_call x1, Pallas kernels: 16.6 us -> 16.2 us  [shards(): pl.pallas_call(functools.partial(attend, n, pool // batch), out_shape=plt...]
where the time goes in v5:
time: 17 us; the launch traced here: 16.9 us
  Pallas kernels  16.2 us (95%)
  local copies, waits for them, and re-layouts  0.62 us (4%)
    pallas_call x1, Pallas kernels, shards(): pl.pallas_call(functools.partial(attend, n, pool // batch), out_shape=plt...  16.2 us
    reshape x1, local copies, waits for them, and re-layouts, shards(): return out.reshape(heads, batch, head_dim).transpose(1, 0, 2)  0.62 us

profile of v5, /device:TPU:0, one launch (start us, length us, event | category | flops | bytes accessed | tf_op | source)
XLA Modules:
  0.0 16.9 jit_solution(334407445290594400)
XLA Ops:
  0.0 16.2 %shard_map.55 = bf16[8,16,128]{2,1,0:T(8,128)(2,1)S(1)} custom-call(bf16[8,16,128]{2,1,0:T(8,128)(2,1)} %q_hbm.1, bf16[32,4,128,128]{3,2,1,0:T(8,128)(2,1)} %k_hbm.1, bf16[32,4,128,128]{3,2,1,0:T(8,128)(2,1)} %v_hbm.1, s32[256]{0:T(256)} %pt_hbm.1, s32[8]{0:T(128)} %len_hbm.1), custom_call_target="tpu_custom_call" | custom-call | tf_op jit(solution)/shard_map/pallas_call | solution.py:246
  16.2 0.6 %copy.8 = bf16[16,8,128]{2,0,1:T(8,128)(2,1)} copy(bf16[16,8,128]{2,1,0:T(8,128)(2,1)S(1)} %bitcast.4) | data formatting | bytes 65536 | tf_op jit(solution)/shard_map/reshape | solution.py:270
